TPU v7x, 128 devices: a whole 4x4x4 slice. The times are simulated.
128 devices in a mesh: sub: 32 (over y, x, core), grp: 4 (over z).
Axes of the slice: x: 4, y: 4, z: 4, core: 2. Of those that a mesh axis runs over, the one named last changes fastest.
Arguments:
- coupling: float32 [128, 2, 256, 8192], P(('sub', 'grp')), may hold values from -6 to 6
- sketch_matrix: float32 [64, 8192], replicated, may hold values from -0.0625 to 0.0625
- block_rows: int32 [128, 2], P(('sub', 'grp')), may hold values from 128 to 256
- members: int32 [32, 8], replicated, may hold values from 0 to 255, as said below
Outputs:
- bases: float32 [32, 16384], P('sub', 'grp')
- projections: float32 [128, 2, 64, 8192], P(('sub', 'grp'))
Inputs may be any that keep to these rules, and one draw needn't show every extreme that they name: `members`: every block number 2 s + k, with s below 128 and k 0 or 1, stands exactly once in the table.
All inputs are finite; a program needn't handle non-finite values.
Results may differ from a plain program's by a relative error of at most 0.000094.
Values sent between devices are 32-bit elements; how exact they have to be, the bound alone decides.
A program may use at most 128 MiB of HBM per device.

v0:
```python
import jax
import jax.numpy as jnp
from jax import lax
from jax.sharding import PartitionSpec as P


def in_blocks(shard, dim, length):
    before, after = (shard.shape[:dim], shard.shape[dim + 1 :])
    return jnp.moveaxis(shard.reshape(*before, length, -1, *after), dim, 0)


def sum_at_owner(shard, axis, dim):
    blocks = in_blocks(shard, dim, lax.axis_size(axis))
    arrived = lax.all_to_all(blocks, axis, split_axis=0, concat_axis=0, tiled=True)
    return arrived.sum(axis=0)


def from_everyone(shard, axis):
    copies = jnp.broadcast_to(shard, (lax.axis_size(axis), *shard.shape))
    return lax.all_to_all(copies, axis, split_axis=0, concat_axis=0, tiled=True)


def taken_together(shard, axis):
    everything = from_everyone(shard, axis)
    return jnp.sum(everything, axis=0)


def joined_along(blocks, dim):
    blocks = jnp.moveaxis(blocks, 0, dim)
    shape = blocks.shape
    return blocks.reshape(*shape[:dim], shape[dim] * shape[dim + 1], *shape[dim + 2 :])


def gather_directly(shard, axis, dim):
    return joined_along(from_everyone(shard, axis), dim)


def block_onehot(members, block_ids):
    matches = members[None, :, :] == block_ids.reshape(-1, 1, 1)
    return (
        jnp.any(matches, axis=2).astype(jnp.float32).reshape(block_ids.shape + (members.shape[0],))
    )


def inverse_lower(factor):
    identity = jnp.eye(factor.shape[-1], dtype=jnp.float32)
    return jax.vmap(lambda single: jax.scipy.linalg.solve_triangular(single, identity, lower=True))(
        factor
    )


def on_device(coupling, sketch_matrix, block_rows, members):
    group_size = lax.axis_size("grp")
    sub_size = lax.axis_size("sub")
    sub_rank = lax.axis_index("sub")
    row_count = coupling.shape[2]
    sketch_width = sketch_matrix.shape[0]
    part_rows = row_count // group_size
    interfaces = members.shape[0]
    local_ifaces = interfaces // sub_size
    positions = lax.iota(jnp.int32, row_count)
    row_mask = (positions[None, :] < block_rows[0][:, None]).astype(jnp.float32)
    sketches = jnp.einsum(
        "krn,cn->krc", coupling[0], sketch_matrix, precision=lax.Precision.HIGHEST
    )
    sketches = sketches * row_mask[:, :, None]
    pieces = sketches.reshape(2, group_size, part_rows * sketch_width)
    block_pair = lax.iota(jnp.int32, 2)
    source_rank = lax.iota(jnp.int32, group_size)
    group_ids = 2 * (sub_rank * group_size + source_rank)[None, :] + block_pair[:, None]
    group_hot = block_onehot(members, group_ids)
    arrived = lax.all_to_all(pieces, "grp", split_axis=1, concat_axis=1, tiled=True)
    spread = jnp.einsum("kgi,kgx->ix", group_hot, arrived, precision=lax.Precision.HIGHEST)
    summed = sum_at_owner(spread, "sub", 0)
    interface_part = summed.reshape(local_ifaces, part_rows, sketch_width)
    gram_part = jnp.einsum(
        "lrc,lrd->lcd", interface_part, interface_part, precision=lax.Precision.HIGHEST
    )
    gram_total = taken_together(gram_part, "grp")
    factor = jnp.linalg.cholesky(gram_total)
    inverse = inverse_lower(factor)
    basis_part = jnp.einsum(
        "lrc,ldc->lrd", interface_part, inverse, precision=lax.Precision.HIGHEST
    )
    basis_flat = basis_part.reshape(local_ifaces, part_rows * sketch_width)
    quarter = gather_directly(basis_flat, "sub", 0)
    picked = jnp.einsum("kgi,ix->kgx", group_hot, quarter, precision=lax.Precision.HIGHEST)
    chosen = lax.all_to_all(picked, "grp", split_axis=1, concat_axis=1, tiled=True)
    chosen = chosen.reshape(2, row_count, sketch_width) * row_mask[:, :, None]
    projections = jnp.einsum("krc,krn->kcn", chosen, coupling[0], precision=lax.Precision.HIGHEST)
    return (basis_flat, projections[None])


def solution(mesh):
    placed = (P(("sub", "grp"), None, None, None), P(), P(("sub", "grp"), None), P())
    return jax.shard_map(
        on_device,
        mesh=mesh,
        in_specs=placed,
        out_specs=(P("sub", "grp"), P(("sub", "grp"), None, None, None)),
        check_vma=False,
    )
```

profile of v0, /device:TPU:1, one launch (start us, length us, event | category | flops | bytes accessed | tf_op | source)
XLA Modules:
  0.0 117.6 jit_solution(10823502988822170092)
XLA Ops:
  0.6 0.0 copy-start
  0.6 0.0 copy-start.1
  0.7 0.9 compare_convert_fusion
  1.5 0.7 copy-done
  2.2 18.8 %fusion.8 = f32[2,256,64]{1,2,0:T(8,128)S(1)} fusion(f32[64,8192]{1,0:T(8,128)S(1)} %copy-done, f32[1,2,256,8192]{3,2,1,0:T(8,128)} %param.4, f32[2,256]{1,0:T(2,128)S(1)} %compare_convert_fusion), kind=kOutput, calls=%fused_computation.7 | convolution fusion | flops 3221258240 | bytes 19007488 | tf_op jit(solution)/shard_map/krn,cn->krc/dot_general | solution.py:63
  21.1 0.1 copy.21
  21.2 0.1 reshape.148
  21.4 0.8 copy.22
  22.1 5.8 %all-to-all-start = ((f32[2,4,4096]{2,0,1:T(2,128)}), f32[2,4,4096]{2,0,1:T(2,128)S(1)}, u32[]{:S(2)}, u32[]{:S(2)}) async-start(f32[2,4,4096]{2,0,1:T(2,128)} %copy.22), calls=%async_computation | async-start | bytes 262144 | tf_op jit(solution)/shard_map/all_to_all | solution.py:72
  28.0 0.1 add.47
  28.1 0.0 copy-done.1
  28.1 0.1 compare_reduce_fusion
  28.2 4.6 %all-to-all-done = f32[2,4,4096]{2,0,1:T(2,128)S(1)} async-done(((f32[2,4,4096]{2,0,1:T(2,128)}), f32[2,4,4096]{2,0,1:T(2,128)S(1)}, u32[]{:S(2)}, u32[]{:S(2)}) %all-to-all-start) | async-done | bytes 131104 | tf_op jit(solution)/shard_map/all_to_all | solution.py:72
  32.8 0.4 convolution_bitcast_fusion
  33.2 0.5 copy.24
  33.8 20.4 %all_to_all.25 = f32[32,1,4096]{2,1,0:T(1,128)S(1)} all-to-all(f32[32,1,4096]{2,1,0:T(1,128)S(1)} %copy.24), channel_id=1, replica_groups=mesh['sub'=32,'grp'=4] {'sub'}, dimensions={0} | all-to-all | bytes 1048576 | tf_op jit(solution)/shard_map/all_to_all | solution.py:14
  54.2 0.4 reduce_sum.20
  54.6 0.1 reshape.150
  54.6 0.2 fusion.24
  54.9 0.1 reshape.160
  55.0 6.8 %all_to_all.26 = f32[4,1,4096]{2,1,0:T(1,128)S(1)} all-to-all(f32[4,1,4096]{2,1,0:T(1,128)S(1)} %reshape.160), channel_id=1, replica_groups=mesh['sub'=32,'grp'=4] {'grp'}, dimensions={0} | all-to-all | bytes 131072 | tf_op jit(solution)/shard_map/all_to_all | solution.py:20
  61.9 0.5 broadcast.88
  62.4 0.8 reduce.11
  63.2 0.1 reshape.161
  63.3 0.1 copy.25
  63.4 0.1 copy.26
  63.5 5.8 %custom-call.8 = f32[1,64,64]{2,1,0:T(8,128)S(1)} custom-call(f32[1,64,64]{2,1,0:T(8,128)S(1)} %fusion.20), custom_call_target="Cholesky" | custom-call | tf_op jit(solution)/shard_map/jit(cholesky)/cholesky | solution.py:80
  69.4 0.6 compare_reduce_fusion.1
  70.1 0.7 fusion.19
  70.7 4.9 %custom-call.9 = f32[1,1,64,64]{2,3,1,0:T(8,128)S(1)} custom-call(f32[1,1,64,64]{3,2,1,0:T(8,128)S(1)} %fusion.19), custom_call_target="InvertDiagBlocksLowerTriangular" | custom-call | tf_op jit(solution)/shard_map/vmap(jit(_solve_triangular))/triangular_solve | solution.py:47
  75.6 0.2 fusion.21
  75.8 0.2 fusion.25
  76.0 0.1 reshape.153
  76.1 0.5 broadcast_in_dim.13
  76.6 16.2 %all_to_all.27 = f32[32,1,4096]{2,1,0:T(1,128)S(1)} all-to-all(f32[32,1,4096]{2,1,0:T(1,128)S(1)} %broadcast_in_dim.13), channel_id=1, replica_groups=mesh['sub'=32,'grp'=4] {'sub'}, dimensions={0} | all-to-all | bytes 1048576 | tf_op jit(solution)/shard_map/all_to_all | solution.py:20
  92.8 1.3 %fusion.13 = f32[2,4,4096]{2,0,1:T(2,128)} fusion(f32[32,1,4096]{2,1,0:T(1,128)S(1)} %all_to_all.27, pred[2,4,32]{2,1,0:T(4,128)(4,1)S(1)} %bitcast.42), kind=kOutput, calls=%fused_computation.8 | convolution fusion | flops 12582912 | bytes 655616 | tf_op jit(solution)/shard_map/kgi,ix->kgx/dot_general | solution.py:87
  94.1 3.3 %all-to-all-start.4 = ((f32[2,4,4096]{2,0,1:T(2,128)}), f32[2,4,4096]{2,0,1:T(2,128)S(1)}, u32[]{:S(2)}, u32[]{:S(2)}) async-start(f32[2,4,4096]{2,0,1:T(2,128)} %fusion.13), calls=%async_computation.4 | async-start | bytes 262144 | tf_op jit(solution)/shard_map/all_to_all | solution.py:88
  97.4 0.7 reshape.152
  98.1 4.1 %all-to-all-done.4 = f32[2,4,4096]{2,0,1:T(2,128)S(1)} async-done(((f32[2,4,4096]{2,0,1:T(2,128)}), f32[2,4,4096]{2,0,1:T(2,128)S(1)}, u32[]{:S(2)}, u32[]{:S(2)}) %all-to-all-start.4) | async-done | bytes 131104 | tf_op jit(solution)/shard_map/all_to_all | solution.py:88
  102.2 0.1 copy.28
  102.3 0.2 reshape.155
  102.5 0.1 copy.29
  102.6 15.0 %fusion.4 = f32[1,2,64,8192]{3,2,1,0:T(8,128)} fusion(f32[1,2,256,8192]{3,2,1,0:T(8,128)} %param.4, f32[2,256,64]{1,2,0:T(8,128)S(1)} %copy.29, f32[2,256]{1,0:T(2,128)S(1)} %compare_convert_fusion), kind=kOutput, calls=%fused_computation.4 | convolution fusion | flops 3221258240 | bytes 21104640 | tf_op jit(solution)/shard_map/krc,krn->kcn/dot_general | solution.py:90
  (6 shorter events, 0.1 us)
Async XLA Ops:
  0.6 1.6 %copy-start = (f32[64,8192]{1,0:T(8,128)S(1)}, f32[64,8192]{1,0:T(8,128)}, u32[]{:S(2)}) copy-start(f32[64,8192]{1,0:T(8,128)} %param.5) | copy-start | bytes 6291460
  0.6 27.4 %copy-start.1 = (s32[32,8]{0,1:T(8,128)S(1)}, s32[32,8]{0,1:T(8,128)}, u32[]{:S(2)}) copy-start(s32[32,8]{0,1:T(8,128)} %param.7) | copy-start | bytes 3076
  22.1 10.7 %all-to-all-start = ((f32[2,4,4096]{2,0,1:T(2,128)}), f32[2,4,4096]{2,0,1:T(2,128)S(1)}, u32[]{:S(2)}, u32[]{:S(2)}) async-start(f32[2,4,4096]{2,0,1:T(2,128)} %copy.22), calls=%async_computation | async-start | bytes 262144 | tf_op jit(solution)/shard_map/all_to_all | solution.py:72
  94.1 8.1 %all-to-all-start.4 = ((f32[2,4,4096]{2,0,1:T(2,128)}), f32[2,4,4096]{2,0,1:T(2,128)S(1)}, u32[]{:S(2)}, u32[]{:S(2)}) async-start(f32[2,4,4096]{2,0,1:T(2,128)} %fusion.13), calls=%async_computation.4 | async-start | bytes 262144 | tf_op jit(solution)/shard_map/all_to_all | solution.py:88
where the time goes:
time: 118 us
  blocking collectives  43.5 us (37%)
  matrix products  36.2 us (31%)
  other arithmetic  14.2 us (12%)
  starting transfers between devices  9.17 us (8%)
  waiting for transfers between devices  8.74 us (7%)
  local copies, waits for them, and re-layouts  4.97 us (4%)
    all_to_all x2, blocking collectives, from_everyone(): return lax.all_to_all(copies, axis, split_axis=0, concat_axis=0, tiled=True)  23.1 us
    all_to_all x1, blocking collectives, sum_at_owner(): lax.all_to_all(blocks, axis, split_axis=0, concat_axis=0, tiled=True)  20.4 us
    dot_general x1, matrix products, on_device(): jnp.einsum('krn,cn->krc', coupling[0], sketch_matrix, precision=lax.Preci...  18.8 us
    dot_general x1, matrix products, on_device(): jnp.einsum('krc,krn->kcn', chosen, coupling[0], precision=lax.Precision.H...  15 us
    another operation x3, other arithmetic, on_device(): factor = jnp.linalg.cholesky(gram_total)  6.52 us
    all_to_all x1, starting transfers between devices, on_device(): lax.all_to_all(pieces, 'grp', split_axis=1, concat_axis=1, tiled=True)  5.85 us
    another operation x2, other arithmetic, inverse_lower(): jax.scipy.linalg.solve_triangular(single, identity, lower=True)  5.55 us
    all_to_all x1, waiting for transfers between devices, on_device(): lax.all_to_all(pieces, 'grp', split_axis=1, concat_axis=1, tiled=True)  4.63 us
  transfers between devices with their start and end apart: 2, of which 2 were waited for; matrix products, arithmetic and copies ran while one was open for 1% of the time, Pallas kernels for 0%

commit v1 on v0

v1 whole, which is shorter than its diff:
```python
import functools

import jax
import jax.numpy as jnp
from jax import lax
from jax.experimental import pallas as pl
from jax.experimental.pallas import tpu as pltpu
from jax.sharding import PartitionSpec as P

MESH = pl.DeviceIdType.MESH
F32 = jnp.float32
BF16 = jnp.bfloat16
LANES = 128
SIDE = 4
RING = [(dy, dx) for dy in range(SIDE) for dx in range(SIDE)]
FAR_FIRST = sorted(range(1, 16), key=lambda r: -sum(min(d, SIDE - d) for d in RING[r]))
NEAR_FIRST = FAR_FIRST[::-1]


def split_two(x):
    high = x.astype(BF16)
    return high, (x - high.astype(F32)).astype(BF16)


def sketch_kernel(c_hbm, s_hbm, rows_ref, out_ref, cbuf, sbuf, sw, pairs, csem, ssem):
    parts, _, part_rows, cols = cbuf.shape
    width = sbuf.shape[0]
    s_copy = pltpu.make_async_copy(s_hbm, sbuf, ssem)
    s_copy.start()

    def load(t, k):
        return pltpu.make_async_copy(
            c_hbm.at[0, k, pl.ds(t * part_rows, part_rows), :], cbuf.at[t, k], csem.at[t, k]
        )

    for t in range(parts):
        for k in range(2):
            load(t, k).start()
    sw[2 * width :, :] = jnp.zeros((256 - 2 * width, cols), BF16)
    s_copy.wait()
    for n in range(0, cols, 1024):
        high, low = split_two(sbuf[:, n : n + 1024])
        sw[:width, n : n + 1024] = high
        sw[width : 2 * width, n : n + 1024] = low

    def body(acc0, acc1):
        accs = (acc0, acc1)
        for a in accs:
            pltpu.matmul_pop(a)

        def quarter(t, carry):
            for k in range(2):
                load(t, k).wait()
            for j in range(cols // 512):
                for m in range(2):
                    n = (2 * j + m) * 256
                    pltpu.matmul_push_rhs(
                        sw[:, n : n + 256], staging_register=0, mxu_index=m, transpose=True
                    )
                    x = jnp.concatenate([cbuf[t, k, :, n : n + 256] for k in range(2)], axis=0)
                    high, low = split_two(x)
                    pltpu.matmul_acc_lhs(accs[m], high, load_staged_rhs=0)
                    pltpu.matmul_acc_lhs(accs[m], low)
            total = pltpu.matmul_pop(acc0)[:, :LANES] + pltpu.matmul_pop(acc1)[:, :LANES]
            total = total + pltpu.roll(total, LANES // 2, 1)
            spot = lax.broadcasted_iota(jnp.int32, (part_rows, LANES), 0) + t * part_rows
            left = lax.broadcasted_iota(jnp.int32, (part_rows // 2, LANES), 1) < LANES // 2
            for k in range(2):
                live = total[k * part_rows : (k + 1) * part_rows]
                pairs[k] = jnp.where(spot < rows_ref[0, k], live, 0.0)
                even = pairs[k, pl.ds(0, part_rows // 2, stride=2), :]
                odd = pairs[k, pl.ds(1, part_rows // 2, stride=2), :]
                out_ref[t, k] = jnp.where(left, even, odd)
            return carry

        lax.fori_loop(0, parts, quarter, 0)

    pl.run_scoped(
        body, pltpu.ACC(0)((2 * part_rows, 256), F32), pltpu.ACC(1)((2 * part_rows, 256), F32)
    )


def sketch_call(coupling, sketch_matrix, block_rows):
    width, cols = sketch_matrix.shape
    return pl.pallas_call(
        sketch_kernel,
        out_shape=jax.ShapeDtypeStruct((4, 2, 32, LANES), F32),
        in_specs=[
            pl.BlockSpec(memory_space=pl.ANY),
            pl.BlockSpec(memory_space=pl.ANY),
            pl.BlockSpec(memory_space=pltpu.SMEM),
        ],
        out_specs=pl.BlockSpec(memory_space=pltpu.VMEM),
        scratch_shapes=[
            pltpu.VMEM((4, 2, 64, cols), F32),
            pltpu.VMEM((width, cols), F32),
            pltpu.VMEM((256, cols), BF16),
            pltpu.VMEM((2, 64, LANES), F32),
            pltpu.SemaphoreType.DMA((4, 2)),
            pltpu.SemaphoreType.DMA,
        ],
        compiler_params=pltpu.CompilerParams(vmem_limit_bytes=40 << 20),
        name="sketch",
    )(coupling, sketch_matrix, block_rows)


def exchange_kernel(
    sk_ref,
    owner_ref,
    pick_ref,
    own_ref,
    zbuf,
    slots,
    rbuf,
    ysend,
    gbuf,
    stage,
    obuf,
    pbuf,
    zsend,
    zrecv,
    rsend,
    rrecv,
    gsend,
    grecv,
    fsend,
    frecv,
    osend,
    orecv,
    psend,
    precv,
):
    s = lax.axis_index("sub")
    g = lax.axis_index("grp")
    core = lax.rem(s, 2)
    chip = s // 2
    y = chip // SIDE
    x = lax.rem(chip, SIDE)
    partner = s + 1 - 2 * core
    other = 1 - core

    def ahead(d):
        return lax.rem(g + d, 4)

    def behind(d):
        return lax.rem(g + 4 - d, 4)

    def chip_to(r):
        dy, dx = RING[r]
        return lax.rem(y + dy, SIDE) * SIDE + lax.rem(x + dx, SIDE)

    def chip_from(r):
        dy, dx = RING[r]
        return lax.rem(y + SIDE - dy, SIDE) * SIDE + lax.rem(x + SIDE - dx, SIDE)

    barrier = pltpu.get_barrier_semaphore()
    peers = [(s, ahead(d)) for d in range(1, 4)]
    peers += [(partner, ahead(d)) for d in range(4)]
    peers += [(chip_to(r) * 2 + core, g) for r in range(1, 16)]
    for peer in peers:
        pl.semaphore_signal(barrier, inc=1, device_id=peer, device_id_type=MESH)
    pl.semaphore_wait(barrier, len(peers))

    def remote(src, dst, send, recv, peer):
        return pltpu.make_async_remote_copy(
            src_ref=src, dst_ref=dst, send_sem=send, recv_sem=recv,
            device_id=peer, device_id_type=MESH,
        )

    def z_copy(d, away):
        return remote(
            sk_ref.at[ahead(d)], zbuf.at[core, g], zsend.at[d, away], zrecv.at[d, away],
            (partner if away else s, ahead(d)),
        )

    z_list = [(d, away) for d in (2, 1, 3) for away in (0, 1)] + [(0, 1)]
    for d, away in z_list:
        z_copy(d, away).start()
    zbuf[core, g] = sk_ref[g]
    for d, away in z_list:
        z_copy(d, away).wait()

    owners = [owner_ref[b] for b in range(16)]

    def r_copy(r):
        return remote(
            slots.at[r], rbuf.at[r], rsend.at[r], rrecv.at[r], (chip_to(r) * 2 + core, g)
        )

    for r in FAR_FIRST + [0]:
        target = chip_to(r) * 2 + core
        total = None
        for b in range(16):
            weight = jnp.where(owners[b] == target, 1.0, 0.0).astype(F32)
            term = zbuf[b // 8, (b % 8) // 2, b % 2] * weight
            total = term if total is None else total + term
        slots[r] = total
        if r:
            r_copy(r).start()
    total = slots[0]
    for r in FAR_FIRST:
        r_copy(r).wait_recv()
    for r in FAR_FIRST:
        total = total + rbuf[r]
    ysend[...] = total
    gbuf[s] = total
    own_ref[g] = total

    def g_copy(r):
        return remote(
            ysend, gbuf.at[s], gsend.at[r], grecv.at[r], (chip_to(r) * 2 + core, g)
        )

    def g_arrived(r):
        i = chip_from(r) * 2 + core
        return remote(
            ysend, gbuf.at[i], gsend.at[r], grecv.at[r], (chip_to(r) * 2 + core, g)
        )

    def f_copy(r):
        i = chip_from(r) * 2 + core
        return remote(
            ysend if r == 0 else gbuf.at[i], gbuf.at[i], fsend.at[r], frecv.at[r], (partner, g)
        )

    def o_copy(d):
        return remote(ysend, obuf.at[g], osend.at[d], orecv.at[d], (s, ahead(d)))

    for r in FAR_FIRST:
        g_copy(r).start()
    f_copy(0).start()
    for d in (2, 1, 3):
        o_copy(d).start()
    for r in NEAR_FIRST:
        g_arrived(r).wait_recv()
        f_copy(r).start()
    for r in range(16):
        f_copy(r).wait_recv()

    def p_copy(d):
        return remote(stage.at[d - 1], pbuf.at[g], psend.at[d], precv.at[d], (s, ahead(d)))

    for d in (2, 1, 3):
        for k in range(2):
            stage[d - 1, k] = gbuf[owner_ref[8 * core + 2 * ahead(d) + k]]
        p_copy(d).start()
    for k in range(2):
        pick_ref[g, k] = gbuf[owner_ref[8 * core + 2 * g + k]]
    for d in (1, 2, 3):
        o_copy(d).wait_recv()
        own_ref[behind(d)] = obuf[behind(d)]
    for d in (1, 3, 2):
        p_copy(d).wait_recv()
        pick_ref[behind(d)] = pbuf[behind(d)]
    for d in range(1, 4):
        o_copy(d).wait_send()
        p_copy(d).wait_send()
    for r in range(16):
        f_copy(r).wait_send()
        if r:
            r_copy(r).wait_send()
            g_copy(r).wait_send()


def exchange_call(sketches, owner):
    piece = (32, LANES)
    dma = pltpu.SemaphoreType.DMA
    return pl.pallas_call(
        exchange_kernel,
        out_shape=(
            jax.ShapeDtypeStruct((4, 2) + piece, F32),
            jax.ShapeDtypeStruct((4,) + piece, F32),
        ),
        in_specs=[
            pl.BlockSpec(memory_space=pltpu.VMEM),
            pl.BlockSpec(memory_space=pltpu.SMEM),
        ],
        out_specs=(
            pl.BlockSpec(memory_space=pltpu.VMEM),
            pl.BlockSpec(memory_space=pltpu.VMEM),
        ),
        scratch_shapes=[
            pltpu.VMEM((2, 4, 2) + piece, F32),
            pltpu.VMEM((16,) + piece, F32),
            pltpu.VMEM((16,) + piece, F32),
            pltpu.VMEM(piece, F32),
            pltpu.VMEM((32,) + piece, F32),
            pltpu.VMEM((3, 2) + piece, F32),
            pltpu.VMEM((4,) + piece, F32),
            pltpu.VMEM((4, 2) + piece, F32),
            dma((4, 2)),
            dma((4, 2)),
            dma((16,)),
            dma((16,)),
            dma((16,)),
            dma((16,)),
            dma((16,)),
            dma((16,)),
            dma((4,)),
            dma((4,)),
            dma((4,)),
            dma((4,)),
        ],
        compiler_params=pltpu.CompilerParams(
            collective_id=0, has_side_effects=True, vmem_limit_bytes=8 << 20
        ),
        name="exchange",
    )(sketches, owner)


def lane_spread(v, lane):
    return jnp.broadcast_to(v[:, lane : lane + 1], v.shape)


def row_spread(v, row):
    return jnp.broadcast_to(v[row : row + 1, :], v.shape)


def inverse_factors(grams):
    size = 64
    row = lax.broadcasted_iota(jnp.int32, (size, size), 0)
    col = lax.broadcasted_iota(jnp.int32, (size, size), 1)
    unit = (row == col).astype(F32)
    inner = lax.broadcasted_iota(jnp.int32, (8, LANES), 0)
    count = len(grams)
    state = []
    for gram in grams:
        wide = jnp.concatenate([gram, unit], axis=1)
        state.append([wide[8 * i : 8 * i + 8] for i in range(8)])
    scales = [[] for _ in grams]
    for p in range(8):
        panels = [
            [[lane_spread(state[a][i], 8 * p + l) for i in range(p, 8)] for l in range(8)]
            for a in range(count)
        ]
        pivots = [jnp.ones((8, LANES), F32) for _ in grams]
        for l in range(8):
            for a in range(count):
                panel = panels[a]
                pivot = row_spread(panel[l][0], l)
                pivots[a] = jnp.where(inner == l, pivot, pivots[a])
                inv = 1.0 / pivot
                times = [v * inv for v in panel[l]]
                times[0] = jnp.where(inner > l, times[0], 0.0)
                for l2 in range(l + 1, 8):
                    element = row_spread(panel[l2][0], l)
                    panel[l2] = [v - t * element for v, t in zip(panel[l2], times)]
                line = row_spread(state[a][p], l)
                for i in range(p, 8):
                    state[a][i] = state[a][i] - times[i - p] * line
        for a in range(count):
            scales[a].append(1.0 / jnp.sqrt(pivots[a]))
    return [
        jnp.concatenate([state[a][i] * scales[a][i] for i in range(8)], axis=0)[:, size:]
        for a in range(count)
    ]


def project_kernel(c_hbm, pick_ref, own_ref, rows_ref, base_ref, out_hbm, cbuf, obuf, full, part, csem, osem):
    cols = cbuf.shape[3]
    rows = cbuf.shape[2]
    wide = cols // 4
    g = lax.axis_index("grp")

    def load(k, j):
        return pltpu.make_async_copy(
            c_hbm.at[0, k, :, pl.ds(j * wide, wide)],
            cbuf.at[0, k, :, pl.ds(j * wide, wide)],
            csem.at[k, j],
        )

    for k in range(2):
        for j in range(4):
            load(k, j).start()
    half = lax.broadcasted_iota(jnp.int32, (32, LANES), 1) < 64

    grams = []
    for a in range(3):
        piece = jnp.concatenate(
            [own_ref[q] if a == 2 else pick_ref[q, a] for q in range(4)], axis=0
        )
        both = lax.dot_general(
            piece, piece, (((0,), (0,)), ((), ())),
            precision=lax.Precision.HIGHEST, preferred_element_type=F32,
        )
        grams.append(both[:64, :64] + both[64:, 64:])
        for q in range(4):
            v = piece[32 * q : 32 * q + 32]
            full[a, pl.ds(64 * q, 32, stride=2), :] = v
            full[a, pl.ds(64 * q + 1, 32, stride=2), :] = pltpu.roll(v, 64, 1)
    inverses = inverse_factors(grams)
    mine = full[2, pl.ds(pl.multiple_of(g * 64, 64), 64), :][:, :64]
    base = lax.dot_general(
        mine, inverses[2], (((1,), (1,)), ((), ())),
        precision=lax.Precision.HIGHEST, preferred_element_type=F32,
    )
    part[...] = jnp.concatenate([base, base], axis=1)
    base_ref[...] = jnp.where(
        half, part[pl.ds(0, 32, stride=2), :], part[pl.ds(1, 32, stride=2), :]
    )

    spot = lax.broadcasted_iota(jnp.int32, (64, rows), 1)
    lefts = []
    for k in range(2):
        turned = lax.dot_general(
            inverses[k], full[k][:, :64], (((1,), (1,)), ((), ())),
            precision=lax.Precision.HIGHEST, preferred_element_type=F32,
        )
        turned = jnp.where(spot < rows_ref[0, k], turned, 0.0)
        lefts.append(jnp.concatenate(split_two(turned), axis=0))

    def store(k, j):
        return pltpu.make_async_copy(
            obuf.at[k, :, pl.ds(j * wide, wide)],
            out_hbm.at[0, k, :, pl.ds(j * wide, wide)],
            osem.at[k, j],
        )

    step = 512
    for k in range(2):
        left = lefts[k]
        for j in range(4):
            load(k, j).wait()
            for n in range(j * wide, (j + 1) * wide, step):
                high, low = split_two(cbuf[0, k, :, n : n + step])
                one = jnp.dot(left, high, preferred_element_type=F32)
                two = jnp.dot(left[:64], low, preferred_element_type=F32)
                obuf[k, :, n : n + step] = one[:64] + one[64:] + two
            store(k, j).start()
    for k in range(2):
        for j in range(4):
            store(k, j).wait()


def project_call(coupling, pick, own, block_rows):
    _, _, rows, cols = coupling.shape
    return pl.pallas_call(
        project_kernel,
        out_shape=(
            jax.ShapeDtypeStruct((32, LANES), F32),
            jax.ShapeDtypeStruct((1, 2, 64, cols), F32),
        ),
        in_specs=[
            pl.BlockSpec(memory_space=pl.ANY),
            pl.BlockSpec(memory_space=pltpu.VMEM),
            pl.BlockSpec(memory_space=pltpu.VMEM),
            pl.BlockSpec(memory_space=pltpu.SMEM),
        ],
        out_specs=(
            pl.BlockSpec(memory_space=pltpu.VMEM),
            pl.BlockSpec(memory_space=pl.ANY),
        ),
        scratch_shapes=[
            pltpu.VMEM((1, 2, rows, cols), F32),
            pltpu.VMEM((2, 64, cols), F32),
            pltpu.VMEM((3, rows, LANES), F32),
            pltpu.VMEM((64, LANES), F32),
            pltpu.SemaphoreType.DMA((2, 4)),
            pltpu.SemaphoreType.DMA((2, 4)),
        ],
        compiler_params=pltpu.CompilerParams(vmem_limit_bytes=40 << 20),
        name="project",
    )(coupling, pick, own, block_rows)


def on_device(coupling, sketch_matrix, block_rows, members):
    chip = lax.axis_index("sub") // 2
    ids = 16 * chip + lax.iota(jnp.int32, 16)
    hit = members[None, :, :] == ids[:, None, None]
    index = lax.broadcasted_iota(jnp.int32, hit.shape, 1)
    owner = jnp.sum(jnp.where(hit, index, 0), axis=(1, 2))
    sketches = sketch_call(coupling, sketch_matrix, block_rows)
    pick, own = exchange_call(sketches, owner)
    bases, projections = project_call(coupling, pick, own, block_rows)
    return (bases.reshape(1, -1), projections)


def solution(mesh):
    placed = (P(("sub", "grp"), None, None, None), P(), P(("sub", "grp"), None), P())
    return jax.shard_map(
        on_device,
        mesh=mesh,
        in_specs=placed,
        out_specs=(P("sub", "grp"), P(("sub", "grp"), None, None, None)),
        check_vma=False,
    )
```

time: 118 us -> 56.2 us (0.48)
  Pallas kernels: 0 us -> 51.9 us
  blocking collectives: 43.5 us -> 0 us
  matrix products: 36.2 us -> 0 us
  other arithmetic: 14.2 us -> 1.13 us
  starting transfers between devices: 9.17 us -> 0 us
  waiting for transfers between devices: 8.74 us -> 0 us
  local copies, waits for them, and re-layouts: 4.97 us -> 2.25 us
    pallas_call x0 -> x3, Pallas kernels: none -> 51.9 us  [the longest x1 30.8 us: exchange_call(): pl.pallas_call(exchange_kernel, out_shape=(jax.ShapeDtypeStruct((4, 2) +...]
    all_to_all x3 -> x0, blocking collectives: 43.5 us -> none  [the longest x2 23.1 us: from_everyone(): return lax.all_to_all(copies, axis, split_axis=0, concat_axis=0, tiled=True)]
    dot_general x6 -> x0, matrix products: 35.9 us -> none  [the longest x1 18.8 us: on_device(): jnp.einsum('krn,cn->krc', coupling[0], sketch_matrix, precision=lax.Preci...]
    another operation x5 -> x0, other arithmetic: 12.1 us -> none  [the longest x3 6.52 us: on_device(): factor = jnp.linalg.cholesky(gram_total)]
    all_to_all x2 -> x0, starting transfers between devices: 9.17 us -> none  [the longest x1 5.85 us: on_device(): lax.all_to_all(pieces, 'grp', split_axis=1, concat_axis=1, tiled=True)]
    all_to_all x2 -> x0, waiting for transfers between devices: 8.74 us -> none  [the longest x1 4.63 us: on_device(): lax.all_to_all(pieces, 'grp', split_axis=1, concat_axis=1, tiled=True)]
    reshape x7 -> x0, local copies, waits for them, and re-layouts: 2.5 us -> none  [the longest x2 0.9 us: on_device(): pieces = sketches.reshape(2, group_size, part_rows * sketch_width)]
    unnamed x6 -> x4, local copies, waits for them, and re-layouts: 0.98 us -> 2.25 us
  transfers between devices with their start and end apart: 2 -> 0, of which waited for: 2 -> 0; matrix products, arithmetic and copies ran while one was open for 1% -> 0% of each run, Pallas kernels for 0% -> 0%
where the time goes in v1:
time: 56.2 us; the launch traced here: 56 us
  Pallas kernels  51.9 us (92%)
  local copies, waits for them, and re-layouts  2.25 us (4%)
  other arithmetic  1.13 us (2%)
  between operations  0.68 us (1%)
    pallas_call x1, Pallas kernels, exchange_call(): pl.pallas_call(exchange_kernel, out_shape=(jax.ShapeDtypeStruct((4, 2) +...  30.8 us
    pallas_call x1, Pallas kernels, project_call(): pl.pallas_call(project_kernel, out_shape=(jax.ShapeDtypeStruct((32, LANES...  12.6 us
    pallas_call x1, Pallas kernels, sketch_call(): pl.pallas_call(sketch_kernel, out_shape=jax.ShapeDtypeStruct((4, 2, 32, L...  8.44 us
    unnamed x4, local copies, waits for them, and re-layouts  2.25 us
    reduce_sum x1, other arithmetic, on_device(): owner = jnp.sum(jnp.where(hit, index, 0), axis=(1, 2))  1.13 us

profile of v1, /device:TPU:1, one launch (start us, length us, event | category | flops | bytes accessed | tf_op | source)
XLA Modules:
  0.0 56.0 jit_solution(12232019889890296350)
XLA Ops:
  0.7 1.1 %select_reduce_fusion.owner_ref = s32[16]{0:T(128)S(1)} fusion(s32[32,8]{0,1:T(8,128)} %param.7, s32[16]{0:T(128)S(1)} %iota_add_fusion), kind=kLoop, calls=%fused_computation | loop fusion | flops 12272 | bytes 1152 | tf_op jit(solution)/shard_map/reduce_sum | solution.py:471
  1.8 0.0 copy-start
  1.8 1.6 %copy-done = f32[64,8192]{1,0:T(8,128)S(1)} copy-done((f32[64,8192]{1,0:T(8,128)S(1)}, f32[64,8192]{1,0:T(8,128)}, u32[]{:S(2)}) %copy-start) | copy-done | bytes 2097176
  3.4 0.0 copy-start.1
  3.4 0.7 %copy-done.1 = s32[1,2]{1,0:T(1,128)S(1)} copy-done((s32[1,2]{1,0:T(1,128)S(1)}, s32[1,2]{1,0:T(1,128)}, u32[]{:S(2)}) %copy-start.1) | copy-done | bytes 32
  4.0 8.4 %sketch.1.sk_ref = f32[4,2,32,128]{3,2,1,0:T(8,128)S(1)} custom-call(f32[1,2,256,8192]{3,2,1,0:T(8,128)} %c_hbm.3, f32[64,8192]{1,0:T(8,128)S(1)} %copy-done, s32[1,2]{1,0:T(1,128)S(1)} %copy-done.1), custom_call_target="tpu_custom_call" | custom-call | tf_op jit(solution)/shard_map/sketch/pallas_call | solution.py:85
  12.5 30.8 %exchange.1 = (f32[4,2,32,128]{3,2,1,0:T(8,128)S(1)}, f32[4,32,128]{2,1,0:T(8,128)S(1)}) custom-call(f32[4,2,32,128]{3,2,1,0:T(8,128)S(1)} %sketch.1.sk_ref, s32[16]{0:T(128)S(1)} %select_reduce_fusion.owner_ref), custom_call_target="tpu_custom_call" | custom-call | tf_op jit(solution)/shard_map/exchange/pallas_call | solution.py:268
  43.3 12.6 %project.1 = (f32[32,128]{1,0:T(8,128)}, f32[1,2,64,8192]{3,2,1,0:T(8,128)}) custom-call(f32[1,2,256,8192]{3,2,1,0:T(8,128)} %c_hbm.3, f32[4,2,32,128]{3,2,1,0:T(8,128)S(1)} %get-tuple-element.6.pick_ref, f32[4,32,128]{2,1,0:T(8,128)S(1)} %get-tuple-element.7.own_ref, s32[1,2]{1,0:T(1,128)S(1)} %copy-done.1), custom_call_target="tpu_custom_call" | custom-call | tf_op jit(solution)/shard_map/project/pallas_call | solution.py:437
  (1 shorter events, 0.0 us)
Async XLA Ops:
  1.8 1.6 %copy-start = (f32[64,8192]{1,0:T(8,128)S(1)}, f32[64,8192]{1,0:T(8,128)}, u32[]{:S(2)}) copy-start(f32[64,8192]{1,0:T(8,128)} %s_hbm.1) | copy-start | bytes 6291460
  3.4 0.7 %copy-start.1 = (s32[1,2]{1,0:T(1,128)S(1)}, s32[1,2]{1,0:T(1,128)}, u32[]{:S(2)}) copy-start(s32[1,2]{1,0:T(1,128)} %rows_ref.3) | copy-start | bytes 28

commit v2 on v1

v2 whole, which is shorter than its diff:
```python
import functools

import jax
import jax.numpy as jnp
from jax import lax
from jax.experimental import pallas as pl
from jax.experimental.pallas import tpu as pltpu
from jax.sharding import PartitionSpec as P

MESH = pl.DeviceIdType.MESH
F32 = jnp.float32
BF16 = jnp.bfloat16
LANES = 128
SIDE = 4
RING = [(dy, dx) for dy in range(SIDE) for dx in range(SIDE)]
FAR_FIRST = sorted(range(1, 16), key=lambda r: -sum(min(d, SIDE - d) for d in RING[r]))
NEAR_FIRST = FAR_FIRST[::-1]


def split_two(x):
    high = x.astype(BF16)
    return high, (x - high.astype(F32)).astype(BF16)


def gather_kernel(
    c_hbm,
    s_hbm,
    rows_hbm,
    members_hbm,
    pick_ref,
    own_ref,
    cbuf,
    sbuf,
    sw,
    pairs,
    rows_ref,
    mbuf,
    owned,
    sk_ref,
    zbuf,
    slots,
    rbuf,
    ysend,
    gbuf,
    stage,
    obuf,
    pbuf,
    csem,
    ssem,
    isem,
    zsend,
    zrecv,
    rsend,
    rrecv,
    gsend,
    grecv,
    fsend,
    frecv,
    osend,
    orecv,
    psend,
    precv,
):
    parts, _, part_rows, cols = cbuf.shape
    width = sbuf.shape[0]
    s = lax.axis_index("sub")
    g = lax.axis_index("grp")
    core = lax.rem(s, 2)
    chip = s // 2
    y = chip // SIDE
    x = lax.rem(chip, SIDE)
    partner = s + 1 - 2 * core

    def ahead(d):
        return lax.rem(g + d, 4)

    def behind(d):
        return lax.rem(g + 4 - d, 4)

    def turn(t):
        return lax.rem(2 + t + t // 2 - 2 * (t // 3), 4)

    def chip_to(r):
        dy, dx = RING[r]
        return lax.rem(y + dy, SIDE) * SIDE + lax.rem(x + dx, SIDE)

    def chip_from(r):
        dy, dx = RING[r]
        return lax.rem(y + SIDE - dy, SIDE) * SIDE + lax.rem(x + SIDE - dx, SIDE)

    s_copy = pltpu.make_async_copy(s_hbm, sbuf, ssem)
    s_copy.start()
    rows_copy = pltpu.make_async_copy(rows_hbm, rows_ref, isem.at[0])
    rows_copy.start()
    members_copy = pltpu.make_async_copy(members_hbm, mbuf, isem.at[1])
    members_copy.start()

    def load(t, k):
        q = ahead(turn(t))
        return pltpu.make_async_copy(
            c_hbm.at[0, k, pl.ds(q * part_rows, part_rows), :], cbuf.at[q, k], csem.at[t, k]
        )

    for t in range(2):
        for k in range(2):
            load(t, k).start()

    barrier = pltpu.get_barrier_semaphore()
    peers = [(s, ahead(d)) for d in range(1, 4)]
    peers += [(partner, ahead(d)) for d in range(4)]
    peers += [(chip_to(r) * 2 + core, g) for r in range(1, 16)]
    for peer in peers:
        pl.semaphore_signal(barrier, inc=1, device_id=peer, device_id_type=MESH)

    sw[2 * width :, :] = jnp.zeros((256 - 2 * width, cols), BF16)
    rows_copy.wait()
    members_copy.wait()
    table = mbuf[...]
    lane = lax.broadcasted_iota(jnp.int32, table.shape, 1)
    owners = [jnp.max(jnp.where(table == 16 * chip + b, lane, 0)) for b in range(16)]
    for b in range(16):
        owned[b] = owners[b]
    s_copy.wait()
    for n in range(0, cols, 1024):
        high, low = split_two(sbuf[:, n : n + 1024])
        sw[:width, n : n + 1024] = high
        sw[width : 2 * width, n : n + 1024] = low
    pl.semaphore_wait(barrier, len(peers))

    def remote(src, dst, send, recv, peer):
        return pltpu.make_async_remote_copy(
            src_ref=src, dst_ref=dst, send_sem=send, recv_sem=recv,
            device_id=peer, device_id_type=MESH,
        )

    def z_copy(t, away):
        q = ahead(turn(t))
        return remote(
            sk_ref.at[t], zbuf.at[core, g], zsend.at[t, away], zrecv.at[t, away],
            (partner if away else s, q),
        )

    def sketch(acc0, acc1):
        accs = (acc0, acc1)
        for a in accs:
            pltpu.matmul_pop(a)

        def quarter(t, carry):
            q = ahead(turn(t))
            for k in range(2):
                load(t, k).wait()

            @pl.when(t < 2)
            def _():
                for k in range(2):
                    load(t + 2, k).start()

            for j in range(cols // 512):
                for m in range(2):
                    n = (2 * j + m) * 256
                    pltpu.matmul_push_rhs(
                        sw[:, n : n + 256], staging_register=0, mxu_index=m, transpose=True
                    )
                    block = jnp.concatenate([cbuf[q, k, :, n : n + 256] for k in range(2)], axis=0)
                    high, low = split_two(block)
                    pltpu.matmul_acc_lhs(accs[m], high, load_staged_rhs=0)
                    pltpu.matmul_acc_lhs(accs[m], low)
            total = pltpu.matmul_pop(acc0)[:, :LANES] + pltpu.matmul_pop(acc1)[:, :LANES]
            total = total + pltpu.roll(total, LANES // 2, 1)
            spot = lax.broadcasted_iota(jnp.int32, (part_rows, LANES), 0) + q * part_rows
            left = lax.broadcasted_iota(jnp.int32, (part_rows // 2, LANES), 1) < LANES // 2
            for k in range(2):
                live = total[k * part_rows : (k + 1) * part_rows]
                pairs[k] = jnp.where(spot < rows_ref[0, k], live, 0.0)
                even = pairs[k, pl.ds(0, part_rows // 2, stride=2), :]
                odd = pairs[k, pl.ds(1, part_rows // 2, stride=2), :]
                sk_ref[t, k] = jnp.where(left, even, odd)
            z_copy(t, 1).start()

            @pl.when(t < 3)
            def _():
                z_copy(t, 0).start()

            return carry

        lax.fori_loop(0, parts, quarter, 0)

    pl.run_scoped(
        sketch, pltpu.ACC(0)((2 * part_rows, 256), F32), pltpu.ACC(1)((2 * part_rows, 256), F32)
    )
    zbuf[core, g] = sk_ref[3]
    for t in range(4):
        z_copy(t, 1).wait()
        if t < 3:
            z_copy(t, 0).wait()

    def r_copy(r):
        return remote(
            slots.at[r], rbuf.at[r], rsend.at[r], rrecv.at[r], (chip_to(r) * 2 + core, g)
        )

    for r in FAR_FIRST + [0]:
        target = chip_to(r) * 2 + core
        total = None
        for b in range(16):
            weight = jnp.where(owners[b] == target, 1.0, 0.0).astype(F32)
            term = zbuf[b // 8, (b % 8) // 2, b % 2] * weight
            total = term if total is None else total + term
        slots[r] = total
        if r:
            r_copy(r).start()
    total = slots[0]
    for r in FAR_FIRST:
        r_copy(r).wait_recv()
    for r in FAR_FIRST:
        total = total + rbuf[r]
    ysend[...] = total
    gbuf[s] = total
    own_ref[g] = total

    def g_copy(r):
        return remote(
            ysend, gbuf.at[s], gsend.at[r], grecv.at[r], (chip_to(r) * 2 + core, g)
        )

    def g_arrived(r):
        i = chip_from(r) * 2 + core
        return remote(
            ysend, gbuf.at[i], gsend.at[r], grecv.at[r], (chip_to(r) * 2 + core, g)
        )

    def f_copy(r):
        i = chip_from(r) * 2 + core
        return remote(
            ysend if r == 0 else gbuf.at[i], gbuf.at[i], fsend.at[r], frecv.at[r], (partner, g)
        )

    def o_copy(d):
        return remote(ysend, obuf.at[g], osend.at[d], orecv.at[d], (s, ahead(d)))

    for r in FAR_FIRST:
        g_copy(r).start()
    f_copy(0).start()
    for d in (2, 1, 3):
        o_copy(d).start()
    for r in NEAR_FIRST:
        g_arrived(r).wait_recv()
        f_copy(r).start()
    for r in range(16):
        f_copy(r).wait_recv()

    def p_copy(d):
        return remote(stage.at[d - 1], pbuf.at[g], psend.at[d], precv.at[d], (s, ahead(d)))

    for d in (2, 1, 3):
        for k in range(2):
            stage[d - 1, k] = gbuf[owned[8 * core + 2 * ahead(d) + k]]
        p_copy(d).start()
    for k in range(2):
        pick_ref[g, k] = gbuf[owned[8 * core + 2 * g + k]]
    for d in (1, 2, 3):
        o_copy(d).wait_recv()
        own_ref[behind(d)] = obuf[behind(d)]
    for d in (1, 3, 2):
        p_copy(d).wait_recv()
        pick_ref[behind(d)] = pbuf[behind(d)]
    for d in range(1, 4):
        o_copy(d).wait_send()
        p_copy(d).wait_send()
    for r in range(16):
        f_copy(r).wait_send()
        if r:
            r_copy(r).wait_send()
            g_copy(r).wait_send()


def gather_call(coupling, sketch_matrix, block_rows, members):
    piece = (32, LANES)
    dma = pltpu.SemaphoreType.DMA
    vmem = pltpu.VMEM
    width, cols = sketch_matrix.shape
    hbm = pl.BlockSpec(memory_space=pltpu.HBM)
    return pl.pallas_call(
        gather_kernel,
        out_shape=(
            jax.ShapeDtypeStruct((4, 2) + piece, F32),
            jax.ShapeDtypeStruct((4,) + piece, F32),
            vmem((4, 2, 64, cols), F32),
        ),
        in_specs=[hbm] * 4,
        out_specs=(pl.BlockSpec(memory_space=vmem),) * 3,
        scratch_shapes=[
            vmem((width, cols), F32),
            vmem((256, cols), BF16),
            vmem((2, 64, LANES), F32),
            pltpu.SMEM((1, 2), jnp.int32),
            vmem((8, 32), jnp.int32),
            pltpu.SMEM((16,), jnp.int32),
            vmem((4, 2) + piece, F32),
            vmem((2, 4, 2) + piece, F32),
            vmem((16,) + piece, F32),
            vmem((16,) + piece, F32),
            vmem(piece, F32),
            vmem((32,) + piece, F32),
            vmem((3, 2) + piece, F32),
            vmem((4,) + piece, F32),
            vmem((4, 2) + piece, F32),
            dma((4, 2)),
            dma,
            dma((2,)),
            dma((4, 2)),
            dma((4, 2)),
            dma((16,)),
            dma((16,)),
            dma((16,)),
            dma((16,)),
            dma((16,)),
            dma((16,)),
            dma((4,)),
            dma((4,)),
            dma((4,)),
            dma((4,)),
        ],
        compiler_params=pltpu.CompilerParams(
            collective_id=0, has_side_effects=True, vmem_limit_bytes=30 << 20
        ),
        name="gather",
    )(coupling, sketch_matrix, block_rows, members)


def lane_spread(v, lane):
    return jnp.broadcast_to(v[:, lane : lane + 1], v.shape)


def row_spread(v, row):
    return jnp.broadcast_to(v[row : row + 1, :], v.shape)


def inverse_factors(grams):
    size = 64
    row = lax.broadcasted_iota(jnp.int32, (size, size), 0)
    col = lax.broadcasted_iota(jnp.int32, (size, size), 1)
    unit = (row == col).astype(F32)
    inner = lax.broadcasted_iota(jnp.int32, (8, LANES), 0)
    count = len(grams)
    state = []
    for gram in grams:
        wide = jnp.concatenate([gram, unit], axis=1)
        state.append([wide[8 * i : 8 * i + 8] for i in range(8)])
    scales = [[] for _ in grams]
    for p in range(8):
        panels = [
            [[lane_spread(state[a][i], 8 * p + l) for i in range(p, 8)] for l in range(8)]
            for a in range(count)
        ]
        pivots = [jnp.ones((8, LANES), F32) for _ in grams]
        for l in range(8):
            for a in range(count):
                panel = panels[a]
                pivot = row_spread(panel[l][0], l)
                pivots[a] = jnp.where(inner == l, pivot, pivots[a])
                inv = 1.0 / pivot
                times = [v * inv for v in panel[l]]
                times[0] = jnp.where(inner > l, times[0], 0.0)
                for l2 in range(l + 1, 8):
                    element = row_spread(panel[l2][0], l)
                    panel[l2] = [v - t * element for v, t in zip(panel[l2], times)]
                line = row_spread(state[a][p], l)
                for i in range(p, 8):
                    state[a][i] = state[a][i] - times[i - p] * line
        for a in range(count):
            scales[a].append(1.0 / jnp.sqrt(pivots[a]))
    return [
        jnp.concatenate([state[a][i] * scales[a][i] for i in range(8)], axis=0)[:, size:]
        for a in range(count)
    ]


def project_kernel(
    cbuf, pick_ref, own_ref, rows_hbm, base_ref, out_hbm, obuf, full, part, rows_ref, osem, isem
):
    parts, _, part_rows, cols = cbuf.shape
    rows = parts * part_rows
    wide = cols // 4
    g = lax.axis_index("grp")
    rows_copy = pltpu.make_async_copy(rows_hbm, rows_ref, isem)
    rows_copy.start()

    half = lax.broadcasted_iota(jnp.int32, (32, LANES), 1) < 64

    grams = []
    for a in range(3):
        piece = jnp.concatenate(
            [own_ref[q] if a == 2 else pick_ref[q, a] for q in range(4)], axis=0
        )
        both = lax.dot_general(
            piece, piece, (((0,), (0,)), ((), ())),
            precision=lax.Precision.HIGHEST, preferred_element_type=F32,
        )
        grams.append(both[:64, :64] + both[64:, 64:])
        for q in range(4):
            v = piece[32 * q : 32 * q + 32]
            full[a, pl.ds(64 * q, 32, stride=2), :] = v
            full[a, pl.ds(64 * q + 1, 32, stride=2), :] = pltpu.roll(v, 64, 1)
    inverses = inverse_factors(grams)
    mine = full[2, pl.ds(pl.multiple_of(g * 64, 64), 64), :][:, :64]
    base = lax.dot_general(
        mine, inverses[2], (((1,), (1,)), ((), ())),
        precision=lax.Precision.HIGHEST, preferred_element_type=F32,
    )
    part[...] = jnp.concatenate([base, base], axis=1)
    base_ref[...] = jnp.where(
        half, part[pl.ds(0, 32, stride=2), :], part[pl.ds(1, 32, stride=2), :]
    )

    rows_copy.wait()
    spot = lax.broadcasted_iota(jnp.int32, (64, rows), 1)
    lefts = []
    for k in range(2):
        turned = lax.dot_general(
            inverses[k], full[k][:, :64], (((1,), (1,)), ((), ())),
            precision=lax.Precision.HIGHEST, preferred_element_type=F32,
        )
        turned = jnp.where(spot < rows_ref[0, k], turned, 0.0)
        lefts.append(jnp.concatenate(split_two(turned), axis=0))

    def store(k, j):
        return pltpu.make_async_copy(
            obuf.at[k, :, pl.ds(j * wide, wide)],
            out_hbm.at[0, k, :, pl.ds(j * wide, wide)],
            osem.at[k, j],
        )

    step = 512
    for k in range(2):
        left = lefts[k]
        for j in range(4):
            for n in range(j * wide, (j + 1) * wide, step):
                high, low = split_two(jnp.concatenate([cbuf[q, k, :, n : n + step] for q in range(parts)], axis=0))
                one = jnp.dot(left, high, preferred_element_type=F32)
                two = jnp.dot(left[:64], low, preferred_element_type=F32)
                obuf[k, :, n : n + step] = one[:64] + one[64:] + two
            store(k, j).start()
    for k in range(2):
        for j in range(4):
            store(k, j).wait()


def project_call(held, pick, own, block_rows):
    parts, _, part_rows, cols = held.shape
    vmem = pltpu.VMEM
    spec = pl.BlockSpec(memory_space=vmem)
    hbm = pl.BlockSpec(memory_space=pltpu.HBM)
    return pl.pallas_call(
        project_kernel,
        out_shape=(
            jax.ShapeDtypeStruct((32, LANES), F32),
            jax.ShapeDtypeStruct((1, 2, 64, cols), F32),
        ),
        in_specs=[spec, spec, spec, hbm],
        out_specs=(spec, hbm),
        scratch_shapes=[
            vmem((2, 64, cols), F32),
            vmem((3, parts * part_rows, LANES), F32),
            vmem((64, LANES), F32),
            pltpu.SMEM((1, 2), jnp.int32),
            pltpu.SemaphoreType.DMA((2, 4)),
            pltpu.SemaphoreType.DMA,
        ],
        compiler_params=pltpu.CompilerParams(vmem_limit_bytes=30 << 20),
        name="project",
    )(held, pick, own, block_rows)


def on_device(coupling, sketch_matrix, block_rows, members):
    hbm = [
        pltpu.with_memory_space_constraint(v, pltpu.HBM)
        for v in (coupling, sketch_matrix, block_rows, members.T)
    ]
    pick, own, held = gather_call(*hbm)
    bases, projections = project_call(held, pick, own, hbm[2])
    return (bases.reshape(1, -1), projections)


def solution(mesh):
    placed = (P(("sub", "grp"), None, None, None), P(), P(("sub", "grp"), None), P())
    return jax.shard_map(
        on_device,
        mesh=mesh,
        in_specs=placed,
        out_specs=(P("sub", "grp"), P(("sub", "grp"), None, None, None)),
        check_vma=False,
    )
```

time: 56.2 us -> 42.7 us (0.76)
  Pallas kernels: 51.9 us -> 41.9 us
  local copies, waits for them, and re-layouts: 2.25 us -> 0 us
  other arithmetic: 1.13 us -> 0 us
    pallas_call x2 -> x1, Pallas kernels: 39.3 us -> 32.9 us  [gather_call(): pl.pallas_call(gather_kernel, out_shape=(jax.ShapeDtypeStruct((4, 2) + pi...]
    pallas_call x1, Pallas kernels: 12.6 us -> 9.05 us  [project_call(): pl.pallas_call(project_kernel, out_shape=(jax.ShapeDtypeStruct((32, LANES...]
    unnamed x4 -> x0, local copies, waits for them, and re-layouts: 2.25 us -> none
    reduce_sum x1 -> x0, other arithmetic: 1.13 us -> none  [on_device(): owner = jnp.sum(jnp.where(hit, index, 0), axis=(1, 2))]
where the time goes in v2:
time: 42.7 us; the launch traced here: 42.6 us
  Pallas kernels  41.9 us (98%)
  between operations  0.64 us (1%)
    pallas_call x1, Pallas kernels, gather_call(): pl.pallas_call(gather_kernel, out_shape=(jax.ShapeDtypeStruct((4, 2) + pi...  32.9 us
    pallas_call x1, Pallas kernels, project_call(): pl.pallas_call(project_kernel, out_shape=(jax.ShapeDtypeStruct((32, LANES...  9.05 us

profile of v2, /device:TPU:1, one launch (start us, length us, event | category | flops | bytes accessed | tf_op | source)
XLA Modules:
  0.0 42.6 jit_solution(9638702805440944933)
XLA Ops:
  0.6 32.9 %gather.1 = (f32[4,2,32,128]{3,2,1,0:T(8,128)S(1)}, f32[4,32,128]{2,1,0:T(8,128)S(1)}, f32[4,2,64,8192]{3,2,1,0:T(8,128)S(1)}) custom-call(f32[1,2,256,8192]{3,2,1,0:T(8,128)} %c_hbm.1, f32[64,8192]{1,0:T(8,128)} %s_hbm.1, s32[1,2]{1,0:T(1,128)} %rows_hbm.3, s32[8,32]{1,0:T(8,128)} %bitcast.2), custom_call_target="tpu_custom_call" | custom-call | tf_op jit(solution)/shard_map/gather/pallas_call | solution.py:283
  33.5 9.0 %project.1 = (f32[32,128]{1,0:T(8,128)}, f32[1,2,64,8192]{3,2,1,0:T(8,128)}) custom-call(f32[4,2,64,8192]{3,2,1,0:T(8,128)S(1)} %get-tuple-element.7.cbuf, f32[4,2,32,128]{3,2,1,0:T(8,128)S(1)} %get-tuple-element.8.pick_ref, f32[4,32,128]{2,1,0:T(8,128)S(1)} %get-tuple-element.9.own_ref, s32[1,2]{1,0:T(1,128)} %rows_hbm.3), custom_call_target="tpu_custom_call" | custom-call | tf_op jit(solution)/shard_map/project/pallas_call | solution.py:454

commit v3 on v0

v3 whole, which is shorter than its diff:
```python
import jax
import jax.numpy as jnp
from jax import lax
from jax.experimental import pallas as pl
from jax.experimental.pallas import tpu as pltpu
from jax.sharding import PartitionSpec as P

MESH = pl.DeviceIdType.MESH
F32 = jnp.float32
BF16 = jnp.bfloat16
LANES = 128
SIDE = 4
RING = [(dy, dx) for dy in range(SIDE) for dx in range(SIDE)]
FAR_FIRST = sorted(range(1, 16), key=lambda r: -sum(min(d, SIDE - d) for d in RING[r]))
NEAR_FIRST = FAR_FIRST[::-1]
PIECES = 4


def split_two(x):
    high = x.astype(BF16)
    return high, (x - high.astype(F32)).astype(BF16)


def split_three(x):
    high = x.astype(BF16)
    rest = x - high.astype(F32)
    middle = rest.astype(BF16)
    return high, middle, (rest - middle.astype(F32)).astype(BF16)


def on_left(shape):
    return lax.broadcasted_iota(jnp.int32, shape, 1) < LANES // 2


def half_turn(v):
    return pltpu.roll(v, LANES // 2, 1)


def lane_spread(v, lane):
    return jnp.broadcast_to(v[:, lane : lane + 1], v.shape)


def row_spread(v, row):
    return jnp.broadcast_to(v[row : row + 1, :], v.shape)


def unpack_rows(piece, store):
    turned = half_turn(piece)
    left = on_left(piece.shape)
    count = piece.shape[0]
    store[pl.ds(0, count, stride=2), :] = jnp.where(left, piece, turned)
    store[pl.ds(1, count, stride=2), :] = jnp.where(left, turned, piece)


def gram_of(rows, turned, acc, mxu):
    high, middle, low = split_three(rows)
    left = on_left(rows.shape)
    right = jnp.concatenate(
        [jnp.where(left, high, middle), jnp.where(left, low, jnp.zeros_like(low))], axis=1
    )
    pltpu.matmul_push_rhs(right, staging_register=0, mxu_index=mxu)
    pltpu.matmul_acc_lhs(acc, jnp.concatenate(split_three(turned), axis=0), load_staged_rhs=0)

    def finish():
        out = pltpu.matmul_pop(acc)
        total = (out[128:192] + out[64:128]) + out[:64]
        total = total[:, LANES:] + total[:, :LANES]
        return total + half_turn(total)

    return finish


def inverse_pair(gram, between):
    left = on_left((8, LANES))
    inner = lax.broadcasted_iota(jnp.int32, (8, LANES), 0)
    lane = lax.rem(lax.broadcasted_iota(jnp.int32, (8, LANES), 1), 64)
    a = [gram[8 * i : 8 * i + 8] for i in range(8)]
    b = [(lane == inner + 8 * i).astype(F32) for i in range(8)]
    scales = []
    for p in range(8):
        panel = [
            [
                jnp.where(left, lane_spread(a[i], 8 * p + l), lane_spread(a[i], 64 + 8 * p + l))
                for i in range(p, 8)
            ]
            for l in range(8)
        ]
        pivots = jnp.ones((8, LANES), F32)
        for l in range(8):
            pivot = row_spread(panel[l][0], l)
            pivots = jnp.where(inner == l, pivot, pivots)
            inv = 1.0 / pivot
            times = [v * inv for v in panel[l]]
            times[0] = jnp.where(inner > l, times[0], 0.0)
            for l2 in range(l + 1, 8):
                element = row_spread(panel[l2][0], l)
                panel[l2] = [v - t * element for v, t in zip(panel[l2], times)]
            line_a, line_b = row_spread(a[p], l), row_spread(b[p], l)
            for i in range(p, 8):
                if p < 7:
                    a[i] = a[i] - times[i - p] * line_a
                b[i] = b[i] - times[i - p] * line_b
            between()
        scales.append(1.0 / jnp.sqrt(pivots))
    return jnp.concatenate([v * c for v, c in zip(b, scales)], axis=0)


def twice_split(v):
    high, low = split_two(v)
    once = jnp.where(on_left(v.shape), high, low)
    return jnp.concatenate([once, once], axis=1)


def gather_kernel(
    c_hbm,
    s_hbm,
    rows_hbm,
    members_hbm,
    pick_ref,
    base_ref,
    high_ref,
    low_ref,
    cbuf,
    sbuf,
    sw,
    pairs,
    rows_ref,
    mbuf,
    ownv,
    owned,
    sk_ref,
    zbuf,
    slots,
    rbuf,
    ysend,
    gbuf,
    stage,
    obuf,
    pbuf,
    full,
    firstsem,
    csem,
    isem,
    zsend,
    zrecv,
    rsend,
    rrecv,
    gsend,
    grecv,
    fsend,
    frecv,
    osend,
    orecv,
    psend,
    precv,
):
    parts, _, part_rows, cols = cbuf.shape
    width = sbuf.shape[0]
    piece = cols // PIECES
    s = lax.axis_index("sub")
    g = lax.axis_index("grp")
    core = lax.rem(s, 2)
    chip = s // 2
    y = chip // SIDE
    x = lax.rem(chip, SIDE)
    partner = s + 1 - 2 * core

    def ahead(d):
        return lax.rem(g + d, 4)

    def behind(d):
        return lax.rem(g + 4 - d, 4)

    def turn(t):
        return lax.rem(2 + t + t // 2 - 2 * (t // 3), 4)

    def chip_to(r):
        dy, dx = RING[r]
        return lax.rem(y + dy, SIDE) * SIDE + lax.rem(x + dx, SIDE)

    def chip_from(r):
        dy, dx = RING[r]
        return lax.rem(y + SIDE - dy, SIDE) * SIDE + lax.rem(x + SIDE - dx, SIDE)

    def remote(src, dst, send, recv, peer):
        return pltpu.make_async_remote_copy(
            src_ref=src, dst_ref=dst, send_sem=send, recv_sem=recv,
            device_id=peer, device_id_type=MESH,
        )

    def first_loads(i):
        span = pl.ds(i * piece, piece)
        q = ahead(turn(0))
        loads = [pltpu.make_async_copy(s_hbm.at[:, span], sbuf.at[:, span], firstsem.at[3 * i])]
        for k in range(2):
            loads.append(
                pltpu.make_async_copy(
                    c_hbm.at[0, k, pl.ds(q * part_rows, part_rows), span],
                    cbuf.at[q, k, :, span],
                    firstsem.at[3 * i + 1 + k],
                )
            )
        return loads

    def load(t, k):
        q = ahead(turn(t))
        return pltpu.make_async_copy(
            c_hbm.at[0, k, pl.ds(q * part_rows, part_rows), :], cbuf.at[q, k], csem.at[t, k]
        )

    for i in range(PIECES):
        for copy in first_loads(i):
            copy.start()
    rows_copy = pltpu.make_async_copy(rows_hbm, rows_ref, isem.at[0])
    rows_copy.start()
    members_copy = pltpu.make_async_copy(members_hbm, mbuf, isem.at[1])
    members_copy.start()
    for k in range(2):
        load(1, k).start()

    barrier = pltpu.get_barrier_semaphore()
    peers = [(s, ahead(d)) for d in range(1, 4)]
    peers += [(partner, ahead(d)) for d in range(4)]
    peers += [(chip_to(r) * 2 + core, g) for r in range(1, 16)]
    for peer in peers:
        pl.semaphore_signal(barrier, inc=1, device_id=peer, device_id_type=MESH)

    def z_copy(t, away):
        return remote(
            sk_ref.at[t], zbuf.at[4 * core + g], zsend, zrecv,
            (partner if away else s, ahead(turn(t))),
        )

    def work(acc0, acc1, gacc, bacc):
        accs = (acc0, acc1)
        for a in (acc0, acc1, gacc, bacc):
            pltpu.matmul_pop(a)
        sw[2 * width :, :] = jnp.zeros((256 - 2 * width, cols), BF16)

        def products(q, start, stop):
            for n in range(start, stop, 256):
                m = n // 256 % 2
                pltpu.matmul_push_rhs(
                    sw[:, n : n + 256], staging_register=0, mxu_index=m, transpose=True
                )
                halves = [split_two(cbuf[q, k, :, n : n + 256]) for k in range(2)]
                for k in range(2):
                    high_ref[q, k, :, n : n + 256] = halves[k][0]
                    low_ref[q, k, :, n : n + 256] = halves[k][1]
                for i in range(2):
                    pltpu.matmul_acc_lhs(
                        accs[m],
                        jnp.concatenate([halves[0][i], halves[1][i]], axis=0),
                        load_staged_rhs=None if i else 0,
                    )

        def finish(t, q):
            total = pltpu.matmul_pop(acc0)[:, :LANES] + pltpu.matmul_pop(acc1)[:, :LANES]
            total = total + half_turn(total)
            spot = lax.broadcasted_iota(jnp.int32, (part_rows, LANES), 0) + q * part_rows
            left = on_left((part_rows // 2, LANES))
            for k in range(2):
                live = total[k * part_rows : (k + 1) * part_rows]
                pairs[k] = jnp.where(spot < rows_ref[0, k], live, 0.0)
                even = pairs[k, pl.ds(0, part_rows // 2, stride=2), :]
                odd = pairs[k, pl.ds(1, part_rows // 2, stride=2), :]
                sk_ref[t, k] = jnp.where(left, even, odd)

        q0 = ahead(turn(0))
        for i in range(PIECES):
            span = slice(i * piece, (i + 1) * piece)
            for copy in first_loads(i):
                copy.wait()
            high, low = split_two(sbuf[:, span])
            sw[:width, span] = high
            sw[width : 2 * width, span] = low
            products(q0, i * piece, (i + 1) * piece)
        for k in range(2):
            load(2, k).start()
        rows_copy.wait()
        finish(0, q0)
        pl.semaphore_wait(barrier, len(peers))
        z_copy(0, 1).start()
        z_copy(0, 0).start()

        members_copy.wait()
        table = mbuf[...]
        lane = lax.broadcasted_iota(jnp.int32, table.shape, 1)
        found = jnp.concatenate(
            [
                jnp.max(jnp.where(table == 16 * chip + b, lane, 0), axis=0, keepdims=True)
                for b in range(16)
            ],
            axis=0,
        )
        ownv[...] = jnp.broadcast_to(jnp.max(found, axis=1, keepdims=True), ownv.shape)
        own_copy = pltpu.make_async_copy(ownv, owned, isem.at[2])
        own_copy.start()

        def quarter(t, carry):
            q = ahead(turn(t))
            for k in range(2):
                load(t, k).wait()

            @pl.when(t < 2)
            def _():
                for k in range(2):
                    load(t + 2, k).start()

            products(q, 0, cols)
            finish(t, q)
            z_copy(t, 1).start()

            @pl.when(t < 3)
            def _():
                z_copy(t, 0).start()

            return carry

        lax.fori_loop(1, parts, quarter, 0)
        own_copy.wait()
        zbuf[4 * core + g] = sk_ref[3]

        def z_all():
            return remote(
                zbuf.at[pl.ds(0, 7)], zbuf.at[pl.ds(0, 7)], zsend, zrecv, (partner, g)
            )

        z_all().wait_recv()
        owners = [owned[b, 0] for b in range(16)]

        def r_copy(r):
            return remote(slots.at[r], rbuf.at[r], rsend, rrecv, (chip_to(r) * 2 + core, g))

        def r_all():
            return remote(
                rbuf.at[pl.ds(1, 15)], rbuf.at[pl.ds(1, 15)], rsend, rrecv, (partner, g)
            )

        for r in FAR_FIRST + [0]:
            target = chip_to(r) * 2 + core
            total = None
            for b in range(16):
                weight = jnp.where(owners[b] == target, 1.0, 0.0).astype(F32)
                term = zbuf[b // 2, b % 2] * weight
                total = term if total is None else total + term
            slots[r] = total
            if r:
                r_copy(r).start()
        total = slots[0]
        r_all().wait_recv()
        for r in FAR_FIRST:
            total = total + rbuf[r]
        ysend[...] = total
        gbuf[s] = total
        obuf[g] = total

        def g_copy(r, i):
            return remote(
                ysend, gbuf.at[i], gsend, grecv.at[r], (chip_to(r) * 2 + core, g)
            )

        def f_copy(r):
            i = chip_from(r) * 2 + core
            return remote(
                ysend if r == 0 else gbuf.at[i], gbuf.at[i], fsend, frecv, (partner, g)
            )

        def f_all():
            return remote(
                gbuf.at[pl.ds(0, 16)], gbuf.at[pl.ds(0, 16)], fsend, frecv, (partner, g)
            )

        def o_copy(d):
            return remote(ysend, obuf.at[g], osend, orecv, (s, ahead(d)))

        def o_all():
            return remote(obuf.at[pl.ds(0, 3)], obuf.at[pl.ds(0, 3)], osend, orecv, (partner, g))

        for r in FAR_FIRST:
            g_copy(r, s).start()
        f_copy(0).start()
        for d in (2, 1, 3):
            o_copy(d).start()
        for r in NEAR_FIRST:
            g_copy(r, chip_from(r) * 2 + core).wait_recv()
            f_copy(r).start()
        f_all().wait_recv()

        def p_copy(d):
            return remote(stage.at[d - 1], pbuf.at[g], psend, precv, (s, ahead(d)))

        def p_all():
            return remote(pbuf.at[pl.ds(0, 3)], pbuf.at[pl.ds(0, 3)], psend, precv, (partner, g))

        for d in (2, 1, 3):
            for k in range(2):
                stage[d - 1, k] = gbuf[owned[8 * core + 2 * ahead(d) + k, 0]]
            p_copy(d).start()
        for k in range(2):
            pbuf[g, k] = gbuf[owned[8 * core + 2 * g + k, 0]]

        o_all().wait_recv()
        for q in range(parts):
            unpack_rows(obuf[q], full.at[pl.ds(q * part_rows, part_rows)])
        rows = full[...]
        gram = gram_of(rows, rows.T[:64], gacc, 0)()
        inverse = inverse_pair(gram, lambda: None)
        mine = full[pl.ds(pl.multiple_of(g * part_rows, part_rows), part_rows), :]
        spread = jnp.concatenate(
            [twice_split(inverse), jnp.zeros((192, 256), BF16)], axis=0
        )
        pltpu.matmul_push_rhs(spread, staging_register=0, mxu_index=1, transpose=True)
        pltpu.matmul_acc_lhs(bacc, jnp.concatenate(split_two(mine), axis=1), load_staged_rhs=0)
        base = pltpu.matmul_pop(bacc)[:, :LANES]
        base = jnp.where(on_left(base.shape), base, half_turn(base))
        pairs[0] = base
        base_ref[...] = jnp.where(
            on_left((32, LANES)),
            pairs[0, pl.ds(0, 32, stride=2), :],
            pairs[0, pl.ds(1, 32, stride=2), :],
        )
        p_all().wait_recv()
        pick_ref[...] = pbuf[...]
        z_all().wait_send()
        r_all().wait_send()
        remote(
            gbuf.at[pl.ds(0, 15)], gbuf.at[pl.ds(0, 15)], gsend, grecv.at[0], (partner, g)
        ).wait_send()
        f_all().wait_send()
        o_all().wait_send()
        p_all().wait_send()

    pl.run_scoped(
        work,
        pltpu.ACC(0)((2 * part_rows, 256), F32),
        pltpu.ACC(1)((2 * part_rows, 256), F32),
        pltpu.ACC(0)((192, 256), F32),
        pltpu.ACC(1)((64, 256), F32),
    )


def gather_call(coupling, sketch_matrix, block_rows, members):
    piece = (32, LANES)
    dma = pltpu.SemaphoreType.DMA
    vmem = pltpu.VMEM
    width, cols = sketch_matrix.shape
    return pl.pallas_call(
        gather_kernel,
        out_shape=(
            jax.ShapeDtypeStruct((4, 2) + piece, F32),
            jax.ShapeDtypeStruct(piece, F32),
            vmem((4, 2, 64, cols), BF16),
            vmem((4, 2, 64, cols), BF16),
        ),
        in_specs=[pl.BlockSpec(memory_space=pltpu.HBM)] * 4,
        out_specs=(pl.BlockSpec(memory_space=vmem),) * 4,
        scratch_shapes=[
            vmem((4, 2, 64, cols), F32),
            vmem((width, cols), F32),
            vmem((256, cols), BF16),
            vmem((2, 64, LANES), F32),
            pltpu.SMEM((1, 2), jnp.int32),
            vmem((8, 32), jnp.int32),
            vmem((16, LANES), jnp.int32),
            pltpu.SMEM((16, LANES), jnp.int32),
            vmem((4, 2) + piece, F32),
            vmem((8, 2) + piece, F32),
            vmem((16,) + piece, F32),
            vmem((16,) + piece, F32),
            vmem(piece, F32),
            vmem((32,) + piece, F32),
            vmem((3, 2) + piece, F32),
            vmem((4,) + piece, F32),
            vmem((4, 2) + piece, F32),
            vmem((256, LANES), F32),
            dma((3 * PIECES,)),
            dma((4, 2)),
            dma((3,)),
            dma,
            dma,
            dma,
            dma,
            dma,
            dma((16,)),
            dma,
            dma,
            dma,
            dma,
            dma,
            dma,
        ],
        compiler_params=pltpu.CompilerParams(
            collective_id=0, has_side_effects=True, vmem_limit_bytes=29 << 20
        ),
        name="gather",
    )(coupling, sketch_matrix, block_rows, members)


def project_kernel(high_ref, low_ref, pick_ref, base_in, rows_hbm, base_ref, out_hbm, obuf, wbuf, full, rows_ref, osem, isem):
    parts, _, part_rows, cols = high_ref.shape
    count = parts * part_rows
    rows_copy = pltpu.make_async_copy(rows_hbm, rows_ref, isem)
    rows_copy.start()
    base_ref[...] = base_in[...]

    def work(*accs):
        grams, wides = accs[:2], accs[2:]
        for a in accs:
            pltpu.matmul_pop(a)
        for k in range(2):
            for q in range(parts):
                unpack_rows(pick_ref[q, k], full.at[k, pl.ds(q * part_rows, part_rows)])
        rows = [full[k] for k in range(2)]
        turned = [v.T[:64] for v in rows]
        ends = [gram_of(rows[k], turned[k], grams[k], k) for k in range(2)]
        rows_copy.wait()
        spot = lax.broadcasted_iota(jnp.int32, (64, count), 1)
        lefts = [
            split_two(jnp.where(spot < rows_ref[0, k], turned[k], 0.0)) for k in range(2)
        ]
        left = on_left((64, LANES))
        gram = jnp.where(left, ends[0](), ends[1]())

        tiles = [(k, n) for k in range(2) for n in range(0, cols, 256)]
        used = [0]

        def accumulator(m):
            used[0] += 1
            pool = wides[m::2]
            return pool[used[0] // 2 % len(pool)]

        waiting = []

        def collect():
            k, n, acc = waiting.pop(0)
            high, low = split_two(pltpu.matmul_pop(acc))
            wbuf[0, k, :, n : n + 256] = high
            wbuf[1, k, :, n : n + 256] = low

        todo = list(tiles)

        def between():
            if not todo:
                return
            k, n = todo.pop(0)
            m = n // 256 % 2
            acc = accumulator(m)
            for i, ref in enumerate((high_ref, low_ref)):
                tile = jnp.concatenate([ref[q, k, :, n : n + 256] for q in range(parts)], axis=0)
                pltpu.matmul_push_rhs(tile, staging_register=i, mxu_index=m)
                pltpu.matmul_acc_lhs(acc, lefts[k][0], load_staged_rhs=i)
                if i == 0:
                    pltpu.matmul_acc_lhs(acc, lefts[k][1])
            waiting.append((k, n, acc))
            if len(waiting) > 4:
                collect()

        both = inverse_pair(gram, between)
        while todo:
            between()
        while waiting:
            collect()
        other = half_turn(both)
        inverses = [jnp.where(left, both, other), jnp.where(left, other, both)]
        stacks = [twice_split(v) for v in inverses]

        def store(k, n, size):
            return pltpu.make_async_copy(
                obuf.at[k, :, pl.ds(n, size)], out_hbm.at[0, k, :, pl.ds(n, size)], osem
            )

        def put():
            k, n, acc = waiting.pop(0)
            obuf[k, :, n : n + 256] = pltpu.matmul_pop(acc)
            if n % 1024 == 768:
                store(k, n - 768, 1024).start()

        for k, n in tiles:
            m = n // 256 % 2
            acc = accumulator(m)
            high, low = wbuf[0, k, :, n : n + 256], wbuf[1, k, :, n : n + 256]
            pltpu.matmul_push_rhs(
                jnp.concatenate([high, high, low, low], axis=0), staging_register=0, mxu_index=m
            )
            pltpu.matmul_acc_lhs(acc, stacks[k], load_staged_rhs=0)
            waiting.append((k, n, acc))
            if len(waiting) > 4:
                put()
        while waiting:
            put()
        pltpu.make_async_copy(obuf, out_hbm.at[0], osem).wait()

    pl.run_scoped(
        work,
        pltpu.ACC(0)((192, 256), F32),
        pltpu.ACC(1)((192, 256), F32),
        *[pltpu.ACC(i % 2)((64, 256), F32) for i in range(16)],
    )


def project_call(high, low, pick, base, block_rows):
    parts, _, part_rows, cols = high.shape
    vmem = pltpu.VMEM
    spec = pl.BlockSpec(memory_space=vmem)
    hbm = pl.BlockSpec(memory_space=pltpu.HBM)
    return pl.pallas_call(
        project_kernel,
        out_shape=(
            jax.ShapeDtypeStruct((32, LANES), F32),
            jax.ShapeDtypeStruct((1, 2, 64, cols), F32),
        ),
        in_specs=[spec, spec, spec, spec, hbm],
        out_specs=(spec, hbm),
        scratch_shapes=[
            vmem((2, 64, cols), F32),
            vmem((2, 2, 64, cols), BF16),
            vmem((2, parts * part_rows, LANES), F32),
            pltpu.SMEM((1, 2), jnp.int32),
            pltpu.SemaphoreType.DMA,
            pltpu.SemaphoreType.DMA,
        ],
        compiler_params=pltpu.CompilerParams(vmem_limit_bytes=29 << 20),
        name="project",
    )(high, low, pick, base, block_rows)


def on_device(coupling, sketch_matrix, block_rows, members):
    hbm = [
        pltpu.with_memory_space_constraint(v, pltpu.HBM)
        for v in (coupling, sketch_matrix, block_rows, members.T)
    ]
    pick, base, high, low = gather_call(*hbm)
    bases, projections = project_call(high, low, pick, base, hbm[2])
    return (bases.reshape(1, -1), projections)


def solution(mesh):
    placed = (P(("sub", "grp"), None, None, None), P(), P(("sub", "grp"), None), P())
    return jax.shard_map(
        on_device,
        mesh=mesh,
        in_specs=placed,
        out_specs=(P("sub", "grp"), P(("sub", "grp"), None, None, None)),
        check_vma=False,
    )
```

time: 118 us -> 40.1 us (0.34)
  blocking collectives: 43.5 us -> 0 us
  Pallas kernels: 0 us -> 39.3 us
  matrix products: 36.2 us -> 0 us
  other arithmetic: 14.2 us -> 0 us
  starting transfers between devices: 9.17 us -> 0 us
  waiting for transfers between devices: 8.74 us -> 0 us
  local copies, waits for them, and re-layouts: 4.97 us -> 0 us
    all_to_all x3 -> x0, blocking collectives: 43.5 us -> none  [the longest x2 23.1 us: from_everyone(): return lax.all_to_all(copies, axis, split_axis=0, concat_axis=0, tiled=True)]
    pallas_call x0 -> x2, Pallas kernels: none -> 39.3 us  [the longest x1 32.4 us: gather_call(): pl.pallas_call(gather_kernel, out_shape=(jax.ShapeDtypeStruct((4, 2) + pi...]
    dot_general x6 -> x0, matrix products: 35.9 us -> none  [the longest x1 18.8 us: on_device(): jnp.einsum('krn,cn->krc', coupling[0], sketch_matrix, precision=lax.Preci...]
    another operation x5 -> x0, other arithmetic: 12.1 us -> none  [the longest x3 6.52 us: on_device(): factor = jnp.linalg.cholesky(gram_total)]
    all_to_all x2 -> x0, starting transfers between devices: 9.17 us -> none  [the longest x1 5.85 us: on_device(): lax.all_to_all(pieces, 'grp', split_axis=1, concat_axis=1, tiled=True)]
    all_to_all x2 -> x0, waiting for transfers between devices: 8.74 us -> none  [the longest x1 4.63 us: on_device(): lax.all_to_all(pieces, 'grp', split_axis=1, concat_axis=1, tiled=True)]
    reshape x7 -> x0, local copies, waits for them, and re-layouts: 2.5 us -> none  [the longest x2 0.9 us: on_device(): pieces = sketches.reshape(2, group_size, part_rows * sketch_width)]
  transfers between devices with their start and end apart: 2 -> 0, of which waited for: 2 -> 0; matrix products, arithmetic and copies ran while one was open for 1% -> 0% of each run, Pallas kernels for 0% -> 0%
where the time goes in v3:
time: 40.1 us; the launch traced here: 39.9 us
  Pallas kernels  39.3 us (98%)
  between operations  0.64 us (2%)
    pallas_call x1, Pallas kernels, gather_call(): pl.pallas_call(gather_kernel, out_shape=(jax.ShapeDtypeStruct((4, 2) + pi...  32.4 us
    pallas_call x1, Pallas kernels, project_call(): pl.pallas_call(project_kernel, out_shape=(jax.ShapeDtypeStruct((32, LANES...  6.86 us

profile of v3, /device:TPU:1, one launch (start us, length us, event | category | flops | bytes accessed | tf_op | source)
XLA Modules:
  0.0 39.9 jit_solution(6266313972847625733)
XLA Ops:
  0.6 32.4 %gather.1 = (f32[4,2,32,128]{3,2,1,0:T(8,128)S(1)}, f32[32,128]{1,0:T(8,128)S(1)}, bf16[4,2,64,8192]{3,2,1,0:T(8,128)(2,1)S(1)}, bf16[4,2,64,8192]{3,2,1,0:T(8,128)(2,1)S(1)}) custom-call(f32[1,2,256,8192]{3,2,1,0:T(8,128)} %c_hbm.1, f32[64,8192]{1,0:T(8,128)} %s_hbm.1, s32[1,2]{1,0:T(1,128)} %rows_hbm.3, s32[8,32]{1,0:T(8,128)} %bitcast.2), custom_call_target="tpu_custom_call" | custom-call | tf_op jit(solution)/shard_map/gather/pallas_call | solution.py:448
  33.1 6.9 %project.1 = (f32[32,128]{1,0:T(8,128)}, f32[1,2,64,8192]{3,2,1,0:T(8,128)}) custom-call(bf16[4,2,64,8192]{3,2,1,0:T(8,128)(2,1)S(1)} %get-tuple-element.8.high_ref, bf16[4,2,64,8192]{3,2,1,0:T(8,128)(2,1)S(1)} %get-tuple-element.9.low_ref, f32[4,2,32,128]{3,2,1,0:T(8,128)S(1)} %get-tuple-element.10.pick_ref, f32[32,128]{1,0:T(8,128)S(1)} %get-tuple-element.11.base_in, ...), custom_call_target="tpu_custom_call" | custom-call | tf_op jit(solution)/shard_map/project/pallas_call | solution.py:607
